TPU v7x, 32 devices: a whole 2x2x4 slice. The times are simulated.
32 devices in a mesh: row: 4 (over z), col: 8 (over y, x, core).
Axes of the slice: x: 2, y: 2, z: 4, core: 2. Of those that a mesh axis runs over, the one named last changes fastest.
Arguments:
- tokens: bfloat16 [24576, 256], P(('row', 'col'))
- codebook: bfloat16 [16384, 256], P(('row', 'col')), may hold values from -6 to 6
- codes: int32 [24576], P(('row', 'col')), may hold values from 0 to 16383
Outputs:
- quantized: bfloat16 [24576, 256], P(('row', 'col'))
- token_loss: float32 [24576], P(('row', 'col'))
- code_counts: int32 [16384], P(('row', 'col'))
- code_loss: float32 [16384], P(('row', 'col'))
- commitment: float32 [], replicated
- perplexity: float32 [], replicated
All inputs are finite; a program needn't handle non-finite values.
Results may differ from a plain program's by a relative error of at most 0.0004.
Values may be sent and summed in bfloat16 or wider, within the bound.
A program may use at most 64 MiB of HBM per device.

v0:
```python
import jax
import jax.numpy as jnp
from jax import lax
from jax.sharding import PartitionSpec as P


def on_device(tokens, codebook, codes):
    tok_rows = tokens.shape[0]
    width = tokens.shape[1]
    per_dev = codebook.shape[0]
    devices = lax.axis_size("row") * lax.axis_size("col")
    total_codes = per_dev * devices
    total_tokens = tok_rows * devices
    full_book = lax.all_gather(codebook, ("row", "col"), axis=0, tiled=True)
    quantized = jnp.take(full_book, codes, axis=0)
    diff = tokens.astype(jnp.float32) - quantized.astype(jnp.float32)
    token_loss = jnp.sum(diff * diff, axis=1) / width
    loss_part = jnp.sum(token_loss)
    local_counts = jax.ops.segment_sum(
        jnp.ones((tok_rows,), jnp.float32), codes, num_segments=total_codes
    )
    local_loss = jax.ops.segment_sum(token_loss, codes, num_segments=total_codes)
    floor_prob = jnp.float32(1.0 / total_tokens)
    totals, loss_totals = lax.psum((local_counts, local_loss), ("row", "col"))
    loss_sum = lax.psum(loss_part, ("row", "col"))
    probs = totals / total_tokens
    terms = jnp.where(
        totals > 0.5, probs * jnp.log(jnp.maximum(probs, floor_prob)), jnp.float32(0.0)
    )
    entropy = jnp.sum(terms)
    offset = lax.axis_index(("row", "col")) * per_dev
    owned_counts = lax.dynamic_slice_in_dim(totals, offset, per_dev, 0)
    code_loss = lax.dynamic_slice_in_dim(loss_totals, offset, per_dev, 0)
    code_counts = owned_counts.astype(jnp.int32)
    commitment = 0.25 * loss_sum / total_tokens
    perplexity = jnp.exp(-entropy)
    return (quantized, token_loss, code_counts, code_loss, commitment, perplexity)


def solution(mesh):
    return jax.shard_map(
        on_device,
        mesh=mesh,
        in_specs=(P(("row", "col"), None), P(("row", "col"), None), P(("row", "col"))),
        out_specs=(
            P(("row", "col"), None),
            P(("row", "col")),
            P(("row", "col")),
            P(("row", "col")),
            P(),
            P(),
        ),
        check_vma=False,
    )
```

profile of v0, /device:TPU:0, one launch (start us, length us, event | category | flops | bytes accessed | tf_op | source)
XLA Modules:
  0.0 242.8 jit_solution(13343456410854663029)
XLA Ops:
  7.2 0.0 all-gather.2.cloned.1.call-start
  7.2 0.7 all-gather.2.cloned.1.call-update
  7.9 0.0 all-reduce.3.cloned.1.call-start
  8.0 5.3 %scatter_custom_fusion = f32[16384]{0:T(1024)} fusion(s32[768]{0:T(1024)} %param.5, f32[768]{0:T(1024)S(1)} %broadcast.9, f32[]{:T(128)} %constant.18.clone.1), kind=kCustom, calls=%fused_computation.8 | custom fusion | flops 768 | bytes 66048 | tf_op jit(solution)/shard_map/scatter-add | solution.py:19
  13.3 0.7 compare_select_fusion
  14.0 0.7 compare_and_fusion
  14.7 76.0 %all-gather.2.cloned.1.call-done = bf16[16384,256]{1,0:T(8,128)(2,1)} async-done(((bf16[512,256]{1,0:T(8,128)(2,1)}), bf16[16384,256]{1,0:T(8,128)(2,1)}) %all-gather.2.cloned.1.call-update) | async-done | bytes 8388624 | tf_op jit(solution)/shard_map/all_gather | solution.py:14
  90.6 6.6 %gather_fusion = bf16[768,256]{1,0:T(8,128)(2,1)S(1)} fusion(bf16[16384,256]{1,0:T(8,128)(2,1)} %all-gather.2.cloned.1.call-done, s32[1024]{0:T(1024)S(1)} %pad_clamp_fusion), kind=kCustom, calls=%fused_computation | custom fusion | bytes 789504 | tf_op jit(solution)/shard_map/jit(_take)/gather | solution.py:15
  97.2 2.0 multiply_reduce_fusion
  99.2 0.6 fusion.4
  99.8 0.0 copy-start
  99.8 5.3 %scatter_custom_fusion.1 = f32[16384]{0:T(1024)} fusion(s32[768]{0:T(1024)} %param.5, f32[768]{0:T(1024)S(1)} %get-tuple-element.9, f32[]{:T(128)} %constant.18.clone.1), kind=kCustom, calls=%fused_computation.6 | custom fusion | flops 768 | bytes 66048 | tf_op jit(solution)/shard_map/scatter-add | solution.py:22
  105.1 0.0 all-reduce.3.cloned.1.call-update
  105.1 39.6 %psum.23 = f32[]{:T(128)} all-reduce(f32[]{:T(128)} %get-tuple-element.8), channel_id=1, replica_groups=mesh['row'=4,'col'=8] {'row','col'}, use_global_device_ids=true, to_apply=%region_6.7 | all-reduce | flops 1 | bytes 8 | tf_op jit(solution)/shard_map/psum | solution.py:25
  145.3 83.5 %all-reduce.3.cloned.1.call-done = (f32[16384]{0:T(1024)}, f32[16384]{0:T(1024)}) async-done(((f32[16384]{0:T(1024)}, f32[16384]{0:T(1024)}), (f32[16384]{0:T(1024)}, f32[16384]{0:T(1024)})) %all-reduce.3.cloned.1.call-update) | async-done | bytes 131088 | tf_op jit(solution)/shard_map/psum | solution.py:24
  228.9 1.5 select_reduce_fusion
  230.3 1.3 dynamic-slice_convert_fusion
  231.7 1.3 dynamic_slice.7
  233.7 0.0 copy-done
  (2 shorter events, 0.0 us)
Async XLA Ops:
  7.2 83.5 %all-gather.2.cloned.1.call-start = ((), (), s32[]{:S(2)}) async-start(), calls=%async_computation | async-start | bytes 8650752 | tf_op jit(solution)/shard_map/all_gather | solution.py:14
  7.9 221.0 %all-reduce.3.cloned.1.call-start = ((), (), s32[]{:S(2)}) async-start(), calls=%async_computation.1 | async-start | bytes 262144 | tf_op jit(solution)/shard_map/psum | solution.py:24
  99.8 133.9 %copy-start = (f32[768]{0:T(1024)}, f32[768]{0:T(1024)S(1)}, u32[]{:S(2)}) copy-start(f32[768]{0:T(1024)S(1)} %get-tuple-element.9) | copy-start | bytes 9220
Sparse Core Ops, SparseCore 0:
  10.8 79.7 all-gather.1
  105.2 123.5 all-reduce.2
where the time goes:
time: 243 us
  waiting for transfers between devices  160 us (66%)
  blocking collectives  39.6 us (16%)
  between operations  17.7 us (7%)
  other arithmetic  17.4 us (7%)
  local copies, waits for them, and re-layouts  7.89 us (3%)
    psum x1, waiting for transfers between devices, on_device(): totals, loss_totals = lax.psum((local_counts, local_loss), ('row', 'col'))  83.5 us
    all_gather x1, waiting for transfers between devices, on_device(): full_book = lax.all_gather(codebook, ('row', 'col'), axis=0, tiled=True)  76 us
    psum x1, blocking collectives, on_device(): loss_sum = lax.psum(loss_part, ('row', 'col'))  39.6 us
    gather x1, local copies, waits for them, and re-layouts, on_device(): quantized = jnp.take(full_book, codes, axis=0)  6.56 us
    scatter-add x1, other arithmetic, on_device(): jax.ops.segment_sum(jnp.ones((tok_rows,), jnp.float32), codes, num_segmen...  5.32 us
    scatter-add x1, other arithmetic, on_device(): jax.ops.segment_sum(token_loss, codes, num_segments=total_codes)  5.3 us
  transfers between devices with their start and end apart: 2, of which 2 were waited for; matrix products, arithmetic and copies ran while one was open for 3% of the time, Pallas kernels for 0%

commit v1 on v0

--- a/solution.py
+++ b/solution.py
@@ -21,7 +21,7 @@
     )
     local_loss = jax.ops.segment_sum(token_loss, codes, num_segments=total_codes)
     floor_prob = jnp.float32(1.0 / total_tokens)
-    totals, loss_totals = lax.psum((local_counts, local_loss), ("row", "col"))
+    totals, loss_totals = lax.psum(lax.psum((local_counts, local_loss), "col"), "row")
     loss_sum = lax.psum(loss_part, ("row", "col"))
     probs = totals / total_tokens
     terms = jnp.where(

time: 243 us -> 212 us (0.87)
  waiting for transfers between devices: 160 us -> 129 us
    psum x1 -> x2, waiting for transfers between devices: 83.5 us -> 52.3 us  [the longest x1 52.3 us: on_device(): lax.psum((local_counts, local_loss), 'col')]
  transfers between devices with their start and end apart: 2 -> 3, of which waited for: 2 -> 2; matrix products, arithmetic and copies ran while one was open for 3% -> 3% of each run, Pallas kernels for 0% -> 0%
where the time goes in v1:
time: 212 us; the launch traced here: 211 us
  waiting for transfers between devices  129 us (61%)
  blocking collectives  39.6 us (19%)
  other arithmetic  17.4 us (8%)
  between operations  17.4 us (8%)
  local copies, waits for them, and re-layouts  7.88 us (4%)
    all_gather x1, waiting for transfers between devices, on_device(): full_book = lax.all_gather(codebook, ('row', 'col'), axis=0, tiled=True)  76 us
    psum x1, waiting for transfers between devices, on_device(): lax.psum((local_counts, local_loss), 'col')  52.3 us
    psum x1, blocking collectives, on_device(): loss_sum = lax.psum(loss_part, ('row', 'col'))  39.6 us
    gather x1, local copies, waits for them, and re-layouts, on_device(): quantized = jnp.take(full_book, codes, axis=0)  6.56 us
    scatter-add x1, other arithmetic, on_device(): jax.ops.segment_sum(jnp.ones((tok_rows,), jnp.float32), codes, num_segmen...  5.32 us
    scatter-add x1, other arithmetic, on_device(): jax.ops.segment_sum(token_loss, codes, num_segments=total_codes)  5.3 us
  transfers between devices with their start and end apart: 3, of which 2 were waited for; matrix products, arithmetic and copies ran while one was open for 3% of the time, Pallas kernels for 0%

profile of v1, /device:TPU:0, one launch (start us, length us, event | category | flops | bytes accessed | tf_op | source)
XLA Modules:
  0.0 211.3 jit_solution(16074067070323048382)
XLA Ops:
  7.2 0.0 all-gather.2.cloned.1.call-start
  7.2 0.7 all-gather.2.cloned.1.call-update
  7.9 0.0 all-reduce.5.cloned.1.call-start
  8.0 5.3 %scatter_custom_fusion = f32[16384]{0:T(1024)} fusion(s32[768]{0:T(1024)} %param.5, f32[768]{0:T(1024)S(1)} %broadcast.9, f32[]{:T(128)} %constant.18.clone.1), kind=kCustom, calls=%fused_computation.8 | custom fusion | flops 768 | bytes 66048 | tf_op jit(solution)/shard_map/scatter-add | solution.py:19
  13.3 0.7 compare_select_fusion
  14.0 0.7 compare_and_fusion
  14.7 76.0 %all-gather.2.cloned.1.call-done = bf16[16384,256]{1,0:T(8,128)(2,1)} async-done(((bf16[512,256]{1,0:T(8,128)(2,1)}), bf16[16384,256]{1,0:T(8,128)(2,1)}) %all-gather.2.cloned.1.call-update) | async-done | bytes 8388624 | tf_op jit(solution)/shard_map/all_gather | solution.py:14
  90.6 6.6 %gather_fusion = bf16[768,256]{1,0:T(8,128)(2,1)S(1)} fusion(bf16[16384,256]{1,0:T(8,128)(2,1)} %all-gather.2.cloned.1.call-done, s32[1024]{0:T(1024)S(1)} %pad_clamp_fusion), kind=kCustom, calls=%fused_computation | custom fusion | bytes 789504 | tf_op jit(solution)/shard_map/jit(_take)/gather | solution.py:15
  97.2 2.0 multiply_reduce_fusion
  99.2 0.6 fusion.4
  99.8 0.0 copy-start
  99.8 5.3 %scatter_custom_fusion.1 = f32[16384]{0:T(1024)} fusion(s32[768]{0:T(1024)} %param.5, f32[768]{0:T(1024)S(1)} %get-tuple-element.11, f32[]{:T(128)} %constant.18.clone.1), kind=kCustom, calls=%fused_computation.6 | custom fusion | flops 768 | bytes 66048 | tf_op jit(solution)/shard_map/scatter-add | solution.py:22
  105.1 0.0 all-reduce.5.cloned.1.call-update
  105.1 0.0 all-reduce.7.cloned.1.call-start
  105.2 52.3 %all-reduce.5.cloned.1.call-done = (f32[16384]{0:T(1024)}, f32[16384]{0:T(1024)}) async-done(((f32[16384]{0:T(1024)}, f32[16384]{0:T(1024)}), (f32[16384]{0:T(1024)}, f32[16384]{0:T(1024)})) %all-reduce.5.cloned.1.call-update) | async-done | bytes 131088 | tf_op jit(solution)/shard_map/psum | solution.py:24
  157.4 0.0 all-reduce.7.cloned.1.call-update
  157.5 39.6 %psum.39 = f32[]{:T(128)} all-reduce(f32[]{:T(128)} %get-tuple-element.10), channel_id=1, replica_groups=mesh['row'=4,'col'=8] {'row','col'}, use_global_device_ids=true, to_apply=%region_8.9 | all-reduce | flops 1 | bytes 8 | tf_op jit(solution)/shard_map/psum | solution.py:25
  197.7 0.0 all-reduce.7.cloned.1.call-done
  197.7 1.5 select_reduce_fusion
  199.2 1.3 dynamic-slice_convert_fusion
  200.5 1.3 dynamic_slice.7
  202.5 0.0 copy-done
  (2 shorter events, 0.0 us)
Async XLA Ops:
  7.2 83.5 %all-gather.2.cloned.1.call-start = ((), (), s32[]{:S(2)}) async-start(), calls=%async_computation | async-start | bytes 8650752 | tf_op jit(solution)/shard_map/all_gather | solution.py:14
  7.9 149.5 %all-reduce.5.cloned.1.call-start = ((), (), s32[]{:S(2)}) async-start(), calls=%async_computation.1 | async-start | bytes 262144 | tf_op jit(solution)/shard_map/psum | solution.py:24
  99.8 102.7 %copy-start = (f32[768]{0:T(1024)}, f32[768]{0:T(1024)S(1)}, u32[]{:S(2)}) copy-start(f32[768]{0:T(1024)S(1)} %get-tuple-element.11) | copy-start | bytes 9220
  105.1 92.6 %all-reduce.7.cloned.1.call-start = ((), (), s32[]{:S(2)}) async-start(), calls=%async_computation.2 | async-start | bytes 262144 | tf_op jit(solution)/shard_map/psum | solution.py:24
Sparse Core Ops, SparseCore 0:
  10.8 79.7 all-gather.1
  105.2 52.1 all-reduce.4
  159.8 34.0 all-reduce.6
